TPU v7x, 32 devices: a whole 2x2x4 slice. The times are simulated.
32 devices in a mesh: gx: 4 (over x, core), gy: 4 (over z), gz: 2 (over y).
Axes of the slice: x: 2, y: 2, z: 4, core: 2. Of those that a mesh axis runs over, the one named last changes fastest.
Arguments:
- layer_input: bfloat16 [1024, 4096], P('gz', ('gx', 'gy')), may hold values from -6 to 6
- modality: int32 [1024], P('gz'), may hold values 0 or 1
- image_spans: int32 [2, 8], replicated, may hold values from 0 to 1024, as said below
- norm_gain: float32 [2, 4096], P(None, ('gx', 'gy')), may hold values from 0.1 to 1.9
- w_qkv: bfloat16 [3, 4096, 2048], P(None, 'gz', ('gx', 'gy')), as said below
- w_out: bfloat16 [2048, 4096], P(('gx', 'gy'), 'gz'), may hold values from -0.125 to 0.125
- grad_out: bfloat16 [1024, 4096], P('gz', ('gx', 'gy')), may hold values from -6 to 6
Outputs:
- attn_out: bfloat16 [1024, 4096], P('gz', ('gx', 'gy'))
- grad_in: bfloat16 [1024, 4096], P('gz', ('gx', 'gy'))
- grad_qkv: float32 [3, 4096, 2048], P(None, 'gz', ('gx', 'gy'))
- grad_wout: float32 [2048, 4096], P(('gx', 'gy'), 'gz')
- grad_gain: float32 [2, 4096], P(None, ('gx', 'gy'))
Inputs may be any that keep to these rules, and one draw needn't show every extreme that they name: `image_spans`: row 0 holds the first position of each of 8 image spans, in increasing order, and row 1 one past its last; spans are disjoint and none is empty. `w_qkv`: entries are at most 20 * 4096 ** -0.5 in magnitude.
All inputs are finite; a program needn't handle non-finite values. No bound on the sum of `modality` on one device may be relied on, other than what follows from the above.
Results may differ from a plain program's by a relative error of at most 0.035.
The roundings to bfloat16 on the way count: a program that leaves them out, or rounds other values in their place, can miss the bound.
Values may be sent and summed in bfloat16 or wider, within the bound.
A program may use at most 128 MiB of HBM per device.

v0:
```python
import math
import jax
import jax.numpy as jnp
from jax import lax
from jax.sharding import PartitionSpec as P

epsilon = 1e-05
masked_low = -1e30


def span_index(positions, image_spans):
    inside = (positions[:, None] >= image_spans[0][None, :]) & (
        positions[:, None] < image_spans[1][None, :]
    )
    labels = jnp.arange(1, image_spans.shape[1] + 1, dtype=jnp.int32)
    return jnp.sum(jnp.where(inside, labels[None, :], 0), axis=1) - 1


def visible(query_pos, query_span, key_pos, key_span):
    causal = key_pos[None, :] <= query_pos[:, None]
    same_image = (query_span[:, None] == key_span[None, :]) & (query_span[:, None] >= 0)
    return causal | same_image


def per_device(layer_input, modality, image_spans, norm_gain, w_qkv, w_out, grad_out):
    tok_rows, local_width = layer_input.shape
    full_width = local_width * lax.axis_size(("gx", "gy"))
    head_dim = w_qkv.shape[2]
    inputs_f = layer_input.astype(jnp.float32)
    squares = lax.psum(jnp.sum(inputs_f * inputs_f, axis=1), ("gx", "gy"))
    inv_rms = lax.rsqrt(squares / full_width + epsilon)
    row_gain = jnp.where(modality[:, None] == 1, norm_gain[1][None, :], norm_gain[0][None, :])
    scaled = inputs_f * inv_rms[:, None]
    normed = (scaled * row_gain).astype(jnp.bfloat16)
    w_full = lax.all_gather(w_qkv, "gz", axis=1, tiled=True)
    wo_full = lax.all_gather(w_out, "gz", axis=1, tiled=True)
    rows_block = w_full
    projected = jnp.einsum(
        "tc,mch->mth",
        lax.all_gather(normed, ("gx", "gy"), axis=1, tiled=True),
        rows_block,
        preferred_element_type=jnp.float32,
    )
    projected = projected.astype(jnp.bfloat16)
    queries = projected[0]
    keys_values = lax.all_gather(
        jnp.concatenate([projected[1], projected[2]], axis=1), "gz", axis=0, tiled=True
    )
    key_total = keys_values.shape[0]
    query_pos = lax.axis_index("gz") * tok_rows + jnp.arange(tok_rows, dtype=jnp.int32)
    query_span = span_index(query_pos, image_spans)
    key_block = 512
    block_count = key_total // key_block
    score_scale = 1.0 / math.sqrt(head_dim)
    block_ids = jnp.arange(block_count, dtype=jnp.int32)

    def block_scores(block_idx):
        first_key = block_idx * key_block
        kv_block = lax.dynamic_slice_in_dim(keys_values, first_key, key_block, 0)
        key_pos = first_key + jnp.arange(key_block, dtype=jnp.int32)
        allowed = visible(query_pos, query_span, key_pos, span_index(key_pos, image_spans))
        scores = (
            lax.dot_general(
                queries,
                kv_block[:, :head_dim],
                (((1,), (1,)), ((), ())),
                preferred_element_type=jnp.float32,
            )
            * score_scale
        )
        return (kv_block, allowed, scores)

    def gather_stats(state, block_idx):
        maxima, summed = state
        kv_block, allowed, scores = block_scores(block_idx)
        new_maxima = jnp.maximum(maxima, jnp.max(jnp.where(allowed, scores, masked_low), axis=1))
        fresh = jnp.sum(jnp.where(allowed, jnp.exp(scores - new_maxima[:, None]), 0.0), axis=1)
        return ((new_maxima, summed * jnp.exp(maxima - new_maxima) + fresh), None)

    start_state = (
        jnp.full((tok_rows,), masked_low, jnp.float32),
        jnp.zeros((tok_rows,), jnp.float32),
    )
    (maxima, summed), unused = lax.scan(gather_stats, start_state, block_ids)
    lse = maxima + jnp.log(summed)

    def block_probs(block_idx):
        kv_block, allowed, scores = block_scores(block_idx)
        return (kv_block, jnp.where(allowed, jnp.exp(scores - lse[:, None]), 0.0))

    def attend(accum, block_idx):
        kv_block, attn_p = block_probs(block_idx)
        return (
            accum
            + jnp.dot(
                attn_p.astype(jnp.bfloat16),
                kv_block[:, head_dim:],
                preferred_element_type=jnp.float32,
            ),
            None,
        )

    attended_f, unused = lax.scan(attend, jnp.zeros((tok_rows, head_dim), jnp.float32), block_ids)
    attended = attended_f.astype(jnp.bfloat16)
    all_heads = lax.all_gather(attended, ("gx", "gy"), axis=1, tiled=True)
    out_rows = lax.all_to_all(wo_full, ("gx", "gy"), split_axis=1, concat_axis=0, tiled=True)
    head_total = out_rows.shape[0] // head_dim
    per_head = jnp.einsum(
        "thd,hdc->htc",
        all_heads.reshape(tok_rows, head_total, head_dim),
        out_rows.reshape(head_total, head_dim, local_width),
        preferred_element_type=jnp.float32,
    )
    per_head = lax.optimization_barrier(per_head.astype(jnp.bfloat16)).astype(jnp.float32)
    attn_out = jnp.sum(per_head, axis=0).astype(jnp.bfloat16)
    segment = lax.all_gather(grad_out, ("gx", "gy"), axis=1, tiled=True)
    d_accum = lax.dot_general(
        segment, wo_full, (((1,), (1,)), ((), ())), preferred_element_type=jnp.float32
    )
    partial_value = lax.dot_general(
        attended, segment, (((0,), (0,)), ((), ())), preferred_element_type=jnp.float32
    )
    d_attended = d_accum.astype(jnp.bfloat16)
    row_dots = jnp.sum(d_attended.astype(jnp.float32) * attended.astype(jnp.float32), axis=1)

    def backward_block(d_query, block_idx):
        kv_block, attn_p = block_probs(block_idx)
        d_probs = lax.dot_general(
            d_attended,
            kv_block[:, head_dim:],
            (((1,), (1,)), ((), ())),
            preferred_element_type=jnp.float32,
        )
        d_scores = (attn_p * (d_probs - row_dots[:, None]) * score_scale).astype(jnp.bfloat16)
        d_query = d_query + jnp.dot(
            d_scores, kv_block[:, :head_dim], preferred_element_type=jnp.float32
        )
        d_keys = lax.dot_general(
            d_scores, queries, (((0,), (0,)), ((), ())), preferred_element_type=jnp.float32
        )
        d_values = lax.dot_general(
            attn_p.astype(jnp.bfloat16),
            d_attended,
            (((0,), (0,)), ((), ())),
            preferred_element_type=jnp.float32,
        )
        return (d_query, jnp.concatenate([d_keys, d_values], axis=1))

    d_query_f, kv_parts = lax.scan(
        backward_block, jnp.zeros((tok_rows, head_dim), jnp.float32), block_ids
    )
    kv_grad = lax.psum_scatter(
        kv_parts.reshape(key_total, 2 * head_dim).astype(jnp.bfloat16),
        "gz",
        scatter_dimension=0,
        tiled=True,
    ).astype(jnp.float32)
    grads = jnp.stack(
        [
            d_query_f.astype(jnp.bfloat16),
            kv_grad[:, :head_dim].astype(jnp.bfloat16),
            kv_grad[:, head_dim:].astype(jnp.bfloat16),
        ]
    )
    w_grad = jnp.einsum(
        "tc,mth->mch",
        lax.all_gather(normed, ("gx", "gy"), axis=1, tiled=True),
        grads,
        preferred_element_type=jnp.float32,
    )
    grad_qkv, grad_wout = (
        lax.psum_scatter(w_grad.astype(jnp.bfloat16), "gz", scatter_dimension=1, tiled=True).astype(
            jnp.float32
        ),
        lax.psum_scatter(
            partial_value.astype(jnp.bfloat16), "gz", scatter_dimension=1, tiled=True
        ).astype(jnp.float32),
    )
    rows_block = w_full
    grad_normed = (
        lax.psum_scatter(
            jnp.einsum("mch,mth->ct", rows_block, grads, preferred_element_type=jnp.float32).astype(
                jnp.bfloat16
            ),
            ("gx", "gy"),
            scatter_dimension=0,
            tiled=True,
        )
        .astype(jnp.float32)
        .T
    )
    upstream = grad_normed * row_gain
    norm_dots = lax.psum(jnp.sum(upstream * scaled, axis=1), ("gx", "gy"))
    grad_in = (inv_rms[:, None] * (upstream - scaled * (norm_dots / full_width)[:, None])).astype(
        jnp.bfloat16
    )
    onehot = (modality[:, None] == jnp.arange(2, dtype=jnp.int32)[None, :]).astype(jnp.float32)
    local_gain = jnp.dot(onehot.T, grad_normed * scaled, precision=lax.Precision.HIGHEST)
    grad_gain = lax.psum(local_gain, "gz")
    return (attn_out, grad_in, grad_qkv, grad_wout, grad_gain)


def solution(mesh):
    in_specs = (
        P("gz", ("gx", "gy")),
        P("gz"),
        P(),
        P(None, ("gx", "gy")),
        P(None, "gz", ("gx", "gy")),
        P(("gx", "gy"), "gz"),
        P("gz", ("gx", "gy")),
    )
    out_specs = (
        P("gz", ("gx", "gy")),
        P("gz", ("gx", "gy")),
        P(None, "gz", ("gx", "gy")),
        P(("gx", "gy"), "gz"),
        P(None, ("gx", "gy")),
    )
    return jax.shard_map(
        per_device, mesh=mesh, in_specs=in_specs, out_specs=out_specs, check_vma=False
    )
```

profile of v0, /device:TPU:0, one launch (start us, length us, event | category | flops | bytes accessed | tf_op | source)
XLA Modules:
  0.0 420.7 jit_solution(4267195177550142330)
XLA Ops:
  10.2 35.2 %psum.21 = f32[512]{0:T(512)S(1)} all-reduce(f32[512]{0:T(512)S(1)} %fusion.65), channel_id=1, replica_groups=mesh['gx'=4,'gy'=4,'gz'=2] {'gx','gy'}, use_global_device_ids=true, to_apply=%region_1.0 | all-reduce | flops 512 | bytes 4096 | tf_op jit(solution)/shard_map/psum | solution.py:30
  48.3 9.5 %all-gather.8.cloned.1.call-done = bf16[3,4096,128]{1,2,0:T(8,128)(2,1)} async-done(((bf16[3,2048,128]{1,2,0:T(8,128)(2,1)}), bf16[3,4096,128]{1,2,0:T(8,128)(2,1)}) %all-gather.8.cloned.1.call-update) | async-done | bytes 3145744 | tf_op jit(solution)/shard_map/all_gather | solution.py:35
  57.8 55.2 %all-gather.6.cloned.1.call-done = bf16[512,4096]{1,0:T(8,128)(2,1)} async-done(((bf16[512,256]{1,0:T(8,128)(2,1)}), bf16[512,4096]{1,0:T(8,128)(2,1)}) %all-gather.6.cloned.1.call-update) | async-done | bytes 4194320 | tf_op jit(solution)/shard_map/all_gather | solution.py:40
  113.0 5.0 %fusion.75 = f32[512,384]{0,1:S(1)} fusion(bf16[512,4096]{1,0:T(8,128)(2,1)} %all-gather.6.cloned.1.call-done, bf16[4096,384]{0,1:T(8,128)(2,1)} %bitcast.156), kind=kOutput, calls=%fused_computation.134 | convolution fusion | flops 1610612736 | bytes 8126464
  118.1 13.9 %all_gather.21 = bf16[1024,256]{0,1:T(8,128)(2,1)S(1)} all-gather(bf16[512,256]{0,1:T(8,128)(2,1)S(1)} %pad_maximum_fusion.1), channel_id=1, replica_groups=mesh['gx'=4,'gy'=4,'gz'=2] {'gz'}, dimensions={0}, use_global_device_ids=true | all-gather | bytes 786432 | tf_op jit(solution)/shard_map/all_gather | solution.py:46
  132.4 4.8 %while.43 = (s32[]{:T(128)}, f32[512]{0:T(512)S(1)}, f32[512]{0:T(512)S(1)}, s32[2]{0:T(128)S(1)}, s32[512]{0:T(512)S(1)}, /*index=5*/s32[2,8]{1,0:T(2,128)S(1)}...) while((s32[]{:T(128)}, f32[512]{0:T(512)S(1)}, ...), condition=%wide.region_7.8_spmd.clone, body=%wide.region_3.7_spmd.clone.sunk | while | flops 70803472 | bytes 2418638 | solution.py:84
  137.7 5.9 %while.44 = (s32[]{:T(128)}, f32[512,128]{1,0:T(8,128)S(1)}, s32[2]{0:T(128)S(1)}, s32[512]{0:T(512)S(1)}, s32[2,8]{1,0:T(2,128)S(1)}, /*index=5*/bf16[1024,256]...) while((s32[]{:T(128)}, f32[512,128]{1,0:T(8,128)S(1)}, ...), condition=%wide.region_10.11_spmd.clone, body=%wide.region_8.10_spmd.clone.sunk | while | flops 136467984 | bytes 945628 | solution.py:103
  143.8 47.6 %all-gather.14.cloned.1.call-done = bf16[512,4096]{1,0:T(8,128)(2,1)} async-done(((bf16[512,256]{1,0:T(8,128)(2,1)}), bf16[512,4096]{1,0:T(8,128)(2,1)}) %all-gather.14.cloned.1.call-update) | async-done | bytes 4194320 | tf_op jit(solution)/shard_map/all_gather | solution.py:116
  191.3 4.0 multiply_reduce_fusion
  196.0 9.3 %while.45 = (s32[]{:T(128)}, f32[512,128]{1,0:T(8,128)S(1)}, bf16[2,512,256]{1,2,0:T(8,128)(2,1)S(1)}, s32[2]{0:T(128)}, s32[512]{0:T(512)S(1)}, /*index=5*/s32[...) while((s32[]{:T(128)}, f32[512,128]{1,0:T(8,128)S(1)}, ...), condition=%wide.region_15.16_spmd.clone, body=%wide.region_13.15_spmd.clone.sunk | while | flops 339367424 | bytes 6974985 | solution.py:149
  206.4 3.9 convolution_convert_fusion.1
  211.1 8.2 %reduce-scatter.5.cloned.1.call-done = bf16[512,256]{1,0:T(8,128)(2,1)} async-done(((bf16[1024,256]{1,0:T(8,128)(2,1)}), bf16[512,256]{1,0:T(8,128)(2,1)}) %reduce-scatter.5.cloned.1.call-update) | async-done | bytes 262160 | tf_op jit(solution)/shard_map/reduce_scatter | solution.py:152
  220.2 5.8 %fusion.52 = bf16[4096,512]{0,1:T(8,128)(2,1)} fusion(bf16[3,4096,128]{1,2,0:T(8,128)(2,1)} %all-gather.8.cloned.1.call-done, bf16[1,512,128]{2,1,0:T(8,128)(2,1)S(1)} %get-tuple-element.678, bf16[1,512,128]{2,1,0:T(8,128)(2,1)S(1)} %get-tuple-element.677, bf16[1,512,128]{2,1,0:T(8,128)(2,1)S(1)} %convert_bitcast_fusion.1), kind=kOutput, calls=%fused_computation.84 | convolution fusion | flops 1613103104 | bytes 7733248 | tf_op jit(solution)/shard_map/mch,mth->ct/dot_general | solution.py:182
  226.3 6.1 %fusion.53 = bf16[3,4096,128]{1,2,0:T(8,128)(2,1)} fusion(bf16[512,4096]{1,0:T(8,128)(2,1)} %all-gather.6.cloned.1.call-done, bf16[1,512,128]{2,1,0:T(8,128)(2,1)S(1)} %get-tuple-element.678, bf16[1,512,128]{2,1,0:T(8,128)(2,1)S(1)} %get-tuple-element.677, bf16[1,512,128]{2,1,0:T(8,128)(2,1)S(1)} %convert_bitcast_fusion.1), kind=kOutput, calls=%fused_computation.85 | convolution fusion | flops 1612578816 | bytes 7733248 | tf_op jit(solution)/shard_map/tc,mth->mch/dot_general | solution.py:165
  233.8 5.5 %all-to-all-start = ((bf16[128,16,256]{2,0,1:T(8,128)(2,1)}), bf16[128,16,256]{2,0,1:T(8,128)(2,1)S(1)}, u32[]{:S(2)}, u32[]{:S(2)}) async-start(bf16[128,16,256]{2,0,1:T(8,128)(2,1)} %copy.51), calls=%async_computation | async-start | bytes 2097152 | tf_op jit(solution)/shard_map/all_to_all | solution.py:106
  239.3 3.1 reduce-scatter.11.cloned.1.call-done
  244.5 25.8 %all-to-all-done = bf16[128,16,256]{2,0,1:T(8,128)(2,1)S(1)} async-done(((bf16[128,16,256]{2,0,1:T(8,128)(2,1)}), bf16[128,16,256]{2,0,1:T(8,128)(2,1)S(1)}, u32[]{:S(2)}, u32[]{:S(2)}) %all-to-all-start) | async-done | bytes 1048608 | tf_op jit(solution)/shard_map/all_to_all | solution.py:106
  270.3 19.1 %all-gather.10.cloned.1.call-done = bf16[512,2048]{0,1:T(8,128)(2,1)} async-done(((bf16[512,128]{0,1:T(8,128)(2,1)}), bf16[512,2048]{0,1:T(8,128)(2,1)}) %all-gather.10.cloned.1.call-update) | async-done | bytes 2097168 | tf_op jit(solution)/shard_map/all_gather | solution.py:105
  289.4 4.8 %convolution_convert_fusion.2 = bf16[16,512,256]{2,1,0:T(8,128)(2,1)} fusion(bf16[512,16,128]{0,2,1:T(8,128)(2,1)} %bitcast.147, bf16[128,16,256]{2,0,1:T(8,128)(2,1)S(1)} %all-to-all-done), kind=kOutput, calls=%fused_computation.88 | convolution fusion | flops 538968064 | bytes 7340032 | tf_op jit(solution)/shard_map/thd,hdc->htc/dot_general | solution.py:108
  294.2 3.5 reduce_sum.98
  297.8 67.0 %reduce-scatter.7.cloned.1.call-done = bf16[256,512]{0,1:T(8,128)(2,1)} async-done(((bf16[4096,512]{0,1:T(8,128)(2,1)}), bf16[256,512]{0,1:T(8,128)(2,1)}) %reduce-scatter.7.cloned.1.call-update) | async-done | bytes 262160 | tf_op jit(solution)/shard_map/reduce_scatter | solution.py:181
  366.1 30.5 %psum.22 = f32[512]{0:T(512)S(1)} all-reduce(f32[512]{0:T(512)S(1)} %fusion.59), channel_id=1, replica_groups=mesh['gx'=4,'gy'=4,'gz'=2] {'gx','gy'}, use_global_device_ids=true, to_apply=%region_19.20 | all-reduce | flops 512 | bytes 4096 | tf_op jit(solution)/shard_map/psum | solution.py:193
  398.1 5.7 %psum.23 = f32[2,256]{1,0:T(2,128)} all-reduce(f32[2,256]{1,0:T(2,128)S(1)} %fusion.63), channel_id=1, replica_groups=mesh['gx'=4,'gy'=4,'gz'=2] {'gz'}, use_global_device_ids=true, to_apply=%region_22.23 | all-reduce | flops 512 | bytes 4096 | tf_op jit(solution)/shard_map/psum | solution.py:199
  403.8 6.4 %reduce-scatter.9.cloned.1.call-done = bf16[3,2048,128]{1,2,0:T(8,128)(2,1)} async-done(((bf16[3,4096,128]{1,2,0:T(8,128)(2,1)}), bf16[3,2048,128]{1,2,0:T(8,128)(2,1)}) %reduce-scatter.9.cloned.1.call-update) | async-done | bytes 1572880 | tf_op jit(solution)/shard_map/reduce_scatter | solution.py:172
  (153 shorter events, 36.5 us)
Async XLA Ops:
  7.2 2.8 copy-start
  7.2 38.2 %copy-start.12 = (s32[512]{0:T(512)S(1)}, s32[512]{0:T(512)}, u32[]{:S(2)}) copy-start(s32[512]{0:T(512)} %param.14) | copy-start | bytes 6148
  7.2 38.2 %copy-start.14 = (f32[2,256]{1,0:T(2,128)S(1)}, f32[2,256]{1,0:T(2,128)}, u32[]{:S(2)}) copy-start(f32[2,256]{1,0:T(2,128)} %param.16) | copy-start | bytes 6148
  7.2 39.2 %copy-start.4 = (bf16[128,2048]{1,0:T(8,128)(2,1)S(1)}, bf16[128,2048]{1,0:T(8,128)(2,1)}, u32[]{:S(2)}) copy-start(bf16[128,2048]{1,0:T(8,128)(2,1)} %param.18) | copy-start | bytes 1572868
  7.2 41.0 %copy-start.5 = (s32[2,8]{1,0:T(2,128)S(1)}, s32[2,8]{1,0:T(2,128)}, u32[]{:S(2)}) copy-start(s32[2,8]{1,0:T(2,128)} %param.15) | copy-start | bytes 196
  7.2 50.6 %all-gather.8.cloned.1.call-start = ((), (), s32[]{:S(2)}) async-start(), calls=%async_computation.6 | async-start | bytes 4718592 | tf_op jit(solution)/shard_map/all_gather | solution.py:35
  10.0 103.0 %all-gather.6.cloned.1.call-start = ((), (), s32[]{:S(2)}) async-start(), calls=%async_computation.5 | async-start | bytes 4456448 | tf_op jit(solution)/shard_map/all_gather | solution.py:40
  45.4 2.8 copy-start.10
  45.4 72.6 %copy-start.6 = (f32[1,256]{1,0:T(1,128)}, f32[1,256]{1,0:T(1,128)S(1)}, u32[]{:S(2)}) copy-start(f32[1,256]{1,0:T(1,128)S(1)} %get-tuple-element.679) | copy-start | bytes 3076
  46.3 97.4 %all-gather.12.cloned.1.call-start = ((), (), s32[]{:S(2)}) async-start(), calls=%async_computation.8 | async-start | bytes 1572864 | tf_op jit(solution)/shard_map/all_gather | solution.py:36
  47.4 143.9 %all-gather.14.cloned.1.call-start = ((), (), s32[]{:S(2)}) async-start(), calls=%async_computation.9 | async-start | bytes 4456448 | tf_op jit(solution)/shard_map/all_gather | solution.py:116
  48.0 171.2 %reduce-scatter.5.cloned.1.call-start = ((), (), s32[]{:S(2)}) async-start(), calls=%async_computation.10 | async-start | bytes 786432 | tf_op jit(solution)/shard_map/reduce_scatter | solution.py:152
  143.7 62.6 %copy-start.2 = (bf16[512,128]{0,1:T(8,128)(2,1)}, bf16[512,128]{0,1:T(8,128)(2,1)S(1)}, u32[]{:S(2)}) copy-start(bf16[512,128]{0,1:T(8,128)(2,1)S(1)} %copy.49) | copy-start | bytes 393220
  206.3 36.1 %reduce-scatter.11.cloned.1.call-start = ((), (), s32[]{:S(2)}) async-start(), calls=%async_computation.13 | async-start | bytes 1572864 | tf_op jit(solution)/shard_map/reduce_scatter | solution.py:175
  210.3 79.1 %all-gather.10.cloned.1.call-start = ((), (), s32[]{:S(2)}) async-start(), calls=%async_computation.7 | async-start | bytes 2228224 | tf_op jit(solution)/shard_map/all_gather | solution.py:105
  211.0 153.8 %reduce-scatter.7.cloned.1.call-start = ((), (), s32[]{:S(2)}) async-start(), calls=%async_computation.11 | async-start | bytes 4456448 | tf_op jit(solution)/shard_map/reduce_scatter | solution.py:181
  226.1 6.4 %copy-start.1 = (bf16[128,4096]{0,1:T(8,128)(2,1)S(1)}, bf16[128,4096]{0,1:T(8,128)(2,1)}, u32[]{:S(2)}) copy-start(bf16[128,4096]{0,1:T(8,128)(2,1)} %all-gather.12.cloned.1.call-done) | copy-start | bytes 3145732
  226.1 184.1 %reduce-scatter.9.cloned.1.call-start = ((), (), s32[]{:S(2)}) async-start(), calls=%async_computation.12 | async-start | bytes 4718592 | tf_op jit(solution)/shard_map/reduce_scatter | solution.py:172
  233.8 36.5 %all-to-all-start = ((bf16[128,16,256]{2,0,1:T(8,128)(2,1)}), bf16[128,16,256]{2,0,1:T(8,128)(2,1)S(1)}, u32[]{:S(2)}, u32[]{:S(2)}) async-start(bf16[128,16,256]{2,0,1:T(8,128)(2,1)} %copy.51), calls=%async_computation | async-start | bytes 2097152 | tf_op jit(solution)/shard_map/all_to_all | solution.py:106
  289.4 75.4 %copy-start.7 = (f32[1,256]{1,0:T(1,128)S(1)}, f32[1,256]{1,0:T(1,128)}, u32[]{:S(2)}) copy-start(f32[1,256]{1,0:T(1,128)} %copy-done.6) | copy-start | bytes 3076
  289.4 75.4 %copy-start.9 = (f32[1,256]{1,0:T(1,128)S(1)}, f32[1,256]{1,0:T(1,128)}, u32[]{:S(2)}) copy-start(f32[1,256]{1,0:T(1,128)} %copy-done.8) | copy-start | bytes 3076
  289.4 75.4 %copy-start.11 = (pred[512]{0:T(512)(128)(4,1)S(1)}, pred[512]{0:T(512)(128)(4,1)}, u32[]{:S(2)}) copy-start(pred[512]{0:T(512)(128)(4,1)} %copy-done.10) | copy-start | bytes 1540
  294.2 102.4 %copy-start.13 = (s32[512]{0:T(512)S(1)}, s32[512]{0:T(512)}, u32[]{:S(2)}) copy-start(s32[512]{0:T(512)} %param.14) | copy-start | bytes 6148
  364.8 48.5 %copy-start.3 = (bf16[256,512]{0,1:T(8,128)(2,1)S(1)}, bf16[256,512]{0,1:T(8,128)(2,1)}, u32[]{:S(2)}) copy-start(bf16[256,512]{0,1:T(8,128)(2,1)} %reduce-scatter.7.cloned.1.call-done) | copy-start | bytes 786436
  (1 other events, 2.7 us)
Sparse Core Ops, SparseCore 0:
  10.1 47.6 all-gather.7
  60.5 52.4 all-gather.5
  115.1 23.5 all-gather.11
  140.6 50.6 all-gather.13
  206.4 12.7 reduce-scatter.4
  221.9 20.3 reduce-scatter.10
  245.1 44.2 all-gather.9
  293.3 71.4 reduce-scatter.6
  367.6 42.5 reduce-scatter.8
where the time goes:
time: 421 us
  waiting for transfers between devices  243 us (58%)
  blocking collectives  85.3 us (20%)
  matrix products  40.2 us (10%)
  local copies, waits for them, and re-layouts  16.1 us (4%)
  between operations  14.2 us (3%)
  other arithmetic  11.5 us (3%)
  starting transfers between devices  6.02 us (1%)
  loops' own time  4.31 us (1%)
    reduce_scatter x1, waiting for transfers between devices, per_device(): lax.psum_scatter(jnp.einsum('mch,mth->ct', rows_block, grads, preferred_e...  67 us
    all_gather x1, waiting for transfers between devices, per_device(): lax.all_gather(normed, ('gx', 'gy'), axis=1, tiled=True)  55.2 us
    all_gather x1, waiting for transfers between devices, per_device(): segment = lax.all_gather(grad_out, ('gx', 'gy'), axis=1, tiled=True)  47.6 us
    psum x1, blocking collectives, per_device(): squares = lax.psum(jnp.sum(inputs_f * inputs_f, axis=1), ('gx', 'gy'))  35.2 us
    psum x1, blocking collectives, per_device(): norm_dots = lax.psum(jnp.sum(upstream * scaled, axis=1), ('gx', 'gy'))  30.5 us
    all_to_all x1, waiting for transfers between devices, per_device(): lax.all_to_all(wo_full, ('gx', 'gy'), split_axis=1, concat_axis=0, tiled=...  25.8 us
    all_gather x1, waiting for transfers between devices, per_device(): all_heads = lax.all_gather(attended, ('gx', 'gy'), axis=1, tiled=True)  19.1 us
    all_gather x1, blocking collectives, per_device(): lax.all_gather(jnp.concatenate([projected[1], projected[2]], axis=1), 'gz...  13.9 us
  transfers between devices with their start and end apart: 10, of which 9 were waited for; matrix products, arithmetic and copies ran while one was open for 11% of the time, Pallas kernels for 0%

commit v1 on v0

--- a/solution.py
+++ b/solution.py
@@ -35,11 +35,44 @@
     w_full = lax.all_gather(w_qkv, "gz", axis=1, tiled=True)
     wo_full = lax.all_gather(w_out, "gz", axis=1, tiled=True)
     rows_block = w_full
-    projected = jnp.einsum(
-        "tc,mch->mth",
-        lax.all_gather(normed, ("gx", "gy"), axis=1, tiled=True),
-        rows_block,
-        preferred_element_type=jnp.float32,
+
+    def clear_slabs(s0, x_local):
+        by_place = []
+        piece_next, e_now, built = (
+            jax.lax.axis_size(("gx", "gy")),
+            jax.lax.axis_index(("gx", "gy")),
+            s0.shape[1],
+        )
+        j0 = 0
+        while j0 < piece_next:
+            by_place.append((j0, (j0 + 1) % piece_next))
+            j0 = j0 + 1
+        all_rows = []
+        j0 = 0
+        while j0 < piece_next:
+            all_rows.append((j0, (j0 - 1) % piece_next))
+            j0 += 1
+        outcome_arr = piece_next // 2
+        answer = reply = s0
+        base_arr = x_local(s0, e_now * built)
+        c = 1
+        while c < outcome_arr + 1:
+            answer = jax.lax.ppermute(answer, ("gx", "gy"), by_place)
+            if c < piece_next - outcome_arr:
+                reply = jax.lax.ppermute(reply, ("gx", "gy"), all_rows)
+                base_arr = base_arr + x_local(reply, (e_now + c) % piece_next * built)
+            base_arr = base_arr + x_local(answer, (e_now - c) % piece_next * built)
+            c = c + 1
+        return base_arr
+
+    projected = clear_slabs(
+        normed,
+        lambda own_block, at: jnp.einsum(
+            "tc,mch->mth",
+            own_block,
+            lax.dynamic_slice_in_dim(rows_block, at, own_block.shape[1], axis=1),
+            preferred_element_type=jnp.float32,
+        ),
     )
     projected = projected.astype(jnp.bfloat16)
     queries = projected[0]

time: 421 us -> 468 us (1.11)
  waiting for transfers between devices: 243 us -> 192 us
  starting transfers between devices: 6.02 us -> 54.7 us
  blocking collectives: 85.3 us -> 131 us
    ppermute x0 -> x15, starting transfers between devices: none -> 54.1 us  [the longest x8 40.2 us: clear_slabs(): answer = jax.lax.ppermute(answer, ('gx', 'gy'), by_place)]
    all_gather x1, waiting for transfers between devices: 47.6 us -> 0.02 us  [per_device(): segment = lax.all_gather(grad_out, ('gx', 'gy'), axis=1, tiled=True)]
    ppermute x0 -> x15, waiting for transfers between devices: none -> 42.7 us  [the longest x8 26.9 us: clear_slabs(): answer = jax.lax.ppermute(answer, ('gx', 'gy'), by_place)]
    all_to_all x0 -> x1, blocking collectives: none -> 41.3 us  [per_device(): lax.all_to_all(wo_full, ('gx', 'gy'), split_axis=1, concat_axis=0, tiled=...]
    all_to_all x1 -> x0, waiting for transfers between devices: 25.8 us -> none  [per_device(): lax.all_to_all(wo_full, ('gx', 'gy'), split_axis=1, concat_axis=0, tiled=...]
    all_gather x1, waiting for transfers between devices: 19.1 us -> 0.01 us  [per_device(): all_heads = lax.all_gather(attended, ('gx', 'gy'), axis=1, tiled=True)]
    dot_general x0 -> x16, matrix products: none -> 9.97 us  [per_device(): jnp.einsum('tc,mch->mth', own_block, lax.dynamic_slice_in_dim(rows_block,...]
    reduce_scatter x1, waiting for transfers between devices: 3.11 us -> 12.9 us  [per_device(): lax.psum_scatter(partial_value.astype(jnp.bfloat16), 'gz', scatter_dimens...]
  transfers between devices with their start and end apart: 10 -> 24, of which waited for: 9 -> 18; matrix products, arithmetic and copies ran while one was open for 11% -> 11% of each run, Pallas kernels for 0% -> 0%
where the time goes in v1:
time: 468 us; the launch traced here: 467 us
  waiting for transfers between devices  192 us (41%)
  blocking collectives  131 us (28%)
  starting transfers between devices  54.7 us (12%)
  matrix products  42 us (9%)
  local copies, waits for them, and re-layouts  15.7 us (3%)
  between operations  14.7 us (3%)
  other arithmetic  12.5 us (3%)
    reduce_scatter x1, waiting for transfers between devices, per_device(): lax.psum_scatter(jnp.einsum('mch,mth->ct', rows_block, grads, preferred_e...  74.6 us
    all_gather x1, waiting for transfers between devices, per_device(): lax.all_gather(normed, ('gx', 'gy'), axis=1, tiled=True)  47.7 us
    all_to_all x1, blocking collectives, per_device(): lax.all_to_all(wo_full, ('gx', 'gy'), split_axis=1, concat_axis=0, tiled=...  41.3 us
    ppermute x8, starting transfers between devices, clear_slabs(): answer = jax.lax.ppermute(answer, ('gx', 'gy'), by_place)  40.2 us
    psum x1, blocking collectives, per_device(): squares = lax.psum(jnp.sum(inputs_f * inputs_f, axis=1), ('gx', 'gy'))  35.2 us
    psum x1, blocking collectives, per_device(): norm_dots = lax.psum(jnp.sum(upstream * scaled, axis=1), ('gx', 'gy'))  30.6 us
    ppermute x8, waiting for transfers between devices, clear_slabs(): answer = jax.lax.ppermute(answer, ('gx', 'gy'), by_place)  26.9 us
    all_gather x1, blocking collectives, per_device(): lax.all_gather(jnp.concatenate([projected[1], projected[2]], axis=1), 'gz...  18.2 us
  transfers between devices with their start and end apart: 24, of which 18 were waited for; matrix products, arithmetic and copies ran while one was open for 11% of the time, Pallas kernels for 0%

profile of v1, /device:TPU:0, one launch (start us, length us, event | category | flops | bytes accessed | tf_op | source)
XLA Modules:
  0.0 467.3 jit_solution(9484943557682374228)
XLA Ops:
  10.2 35.2 %psum.21 = f32[512]{0:T(512)S(1)} all-reduce(f32[512]{0:T(512)S(1)} %fusion.73), channel_id=1, replica_groups=mesh['gx'=4,'gy'=4,'gz'=2] {'gx','gy'}, use_global_device_ids=true, to_apply=%region_1.0 | all-reduce | flops 512 | bytes 4096 | tf_op jit(solution)/shard_map/psum | solution.py:30
  46.8 4.5 collective-permute-start
  51.3 5.3 %collective-permute-done.1 = bf16[512,256]{1,0:T(8,128)(2,1)S(1)} collective-permute-done((bf16[512,256]{1,0:T(8,128)(2,1)S(1)}, bf16[512,256]{1,0:T(8,128)(2,1)S(1)}, u32[]{:S(2)}, u32[]{:S(2)}) %collective-permute-start.1) | collective-permute-done | bytes 262176 | tf_op jit(solution)/shard_map/ppermute | solution.py:60
  83.3 5.7 %collective-permute-done.7 = bf16[512,256]{1,0:T(8,128)(2,1)S(1)} collective-permute-done((bf16[512,256]{1,0:T(8,128)(2,1)S(1)}, bf16[512,256]{1,0:T(8,128)(2,1)S(1)}, u32[]{:S(2)}, u32[]{:S(2)}) %collective-permute-start.7) | collective-permute-done | bytes 262176 | tf_op jit(solution)/shard_map/ppermute | solution.py:60
  89.0 5.2 %collective-permute-start.9 = (bf16[512,256]{1,0:T(8,128)(2,1)S(1)}, bf16[512,256]{1,0:T(8,128)(2,1)S(1)}, u32[]{:S(2)}, u32[]{:S(2)}) collective-permute-start(bf16[512,256]{1,0:T(8,128)(2,1)S(1)} %collective-permute-done.7), channel_id=1, source_target_pairs={{0,2},{2,4},{4,6},{6,8},{8,10},{10,12},{12,14},{14,16},{16,18},{18... | collective-permute-start | bytes 786440 | tf_op jit(solution)/shard_map/ppermute | solution.py:60
  98.6 11.9 %collective-permute-start.11 = (bf16[512,256]{1,0:T(8,128)(2,1)S(1)}, bf16[512,256]{1,0:T(8,128)(2,1)}, u32[]{:S(2)}, u32[]{:S(2)}) collective-permute-start(bf16[512,256]{1,0:T(8,128)(2,1)S(1)} %collective-permute-done.9), channel_id=1, source_target_pairs={{0,2},{2,4},{4,6},{6,8},{8,10},{10,12},{12,14},{14,16},{16,18},{18... | collective-permute-start | bytes 786440 | tf_op jit(solution)/shard_map/ppermute | solution.py:60
  113.8 4.7 %collective-permute-done.11 = bf16[512,256]{1,0:T(8,128)(2,1)} collective-permute-done((bf16[512,256]{1,0:T(8,128)(2,1)S(1)}, bf16[512,256]{1,0:T(8,128)(2,1)}, u32[]{:S(2)}, u32[]{:S(2)}) %collective-permute-start.11) | collective-permute-done | bytes 262176 | tf_op jit(solution)/shard_map/ppermute | solution.py:60
  118.5 8.4 %collective-permute-start.13 = (bf16[512,256]{1,0:T(8,128)(2,1)}, bf16[512,256]{1,0:T(8,128)(2,1)}, u32[]{:S(2)}, u32[]{:S(2)}) collective-permute-start(bf16[512,256]{1,0:T(8,128)(2,1)} %collective-permute-done.11), channel_id=1, source_target_pairs={{0,2},{2,4},{4,6},{6,8},{8,10},{10,12},{12,14},{14,16},{16,18},{18... | collective-permute-start | bytes 786440 | tf_op jit(solution)/shard_map/ppermute | solution.py:60
  132.2 11.9 %collective-permute-start.14 = (bf16[512,256]{1,0:T(8,128)(2,1)}, bf16[512,256]{1,0:T(8,128)(2,1)}, u32[]{:S(2)}, u32[]{:S(2)}) collective-permute-start(bf16[512,256]{1,0:T(8,128)(2,1)} %collective-permute-done.13), channel_id=1, source_target_pairs={{0,2},{2,4},{4,6},{6,8},{8,10},{10,12},{12,14},{14,16},{16,18},{18... | collective-permute-start | bytes 786440 | tf_op jit(solution)/shard_map/ppermute | solution.py:60
  154.3 18.2 %all_gather.19 = bf16[1024,256]{0,1:T(8,128)(2,1)S(1)} all-gather(bf16[512,256]{0,1:T(8,128)(2,1)S(1)} %pad_maximum_fusion.1), channel_id=1, replica_groups=mesh['gx'=4,'gy'=4,'gz'=2] {'gz'}, dimensions={0}, use_global_device_ids=true | all-gather | bytes 786432 | tf_op jit(solution)/shard_map/all_gather | solution.py:79
  172.9 4.8 %while.43 = (s32[]{:T(128)}, f32[512]{0:T(512)S(1)}, f32[512]{0:T(512)S(1)}, s32[2]{0:T(128)S(1)}, s32[512]{0:T(512)S(1)}, /*index=5*/s32[2,8]{1,0:T(2,128)S(1)}...) while((s32[]{:T(128)}, f32[512]{0:T(512)S(1)}, ...), condition=%wide.region_7.8_spmd.clone, body=%wide.region_3.7_spmd.clone.sunk | while | flops 70803472 | bytes 2418646 | solution.py:117
  177.7 4.5 while.44
  186.6 8.0 %while.45 = (s32[]{:T(128)}, f32[512,128]{1,0:T(8,128)S(1)}, bf16[2,512,256]{1,2,0:T(8,128)(2,1)}, s32[2]{0:T(128)S(1)}, s32[512]{0:T(512)S(1)}, /*index=5*/s32[...) while((s32[]{:T(128)}, f32[512,128]{1,0:T(8,128)S(1)}, ...), condition=%wide.region_15.16_spmd.clone, body=%wide.region_13.15_spmd.clone.sunk | while | flops 339367424 | bytes 6974993 | solution.py:182
  201.8 9.2 %reduce-scatter.5.cloned.1.call-done = bf16[512,256]{1,0:T(8,128)(2,1)} async-done(((bf16[1024,256]{1,0:T(8,128)(2,1)}), bf16[512,256]{1,0:T(8,128)(2,1)}) %reduce-scatter.5.cloned.1.call-update) | async-done | bytes 262160 | tf_op jit(solution)/shard_map/reduce_scatter | solution.py:185
  212.0 5.7 %fusion.52 = bf16[4096,512]{0,1:T(8,128)(2,1)} fusion(bf16[3,4096,128]{1,2,0:T(8,128)(2,1)} %all-gather.6.cloned.1.call-done, bf16[1,512,128]{2,1,0:T(8,128)(2,1)S(1)} %get-tuple-element.678, bf16[1,512,128]{2,1,0:T(8,128)(2,1)S(1)} %get-tuple-element.677, bf16[1,512,128]{2,1,0:T(8,128)(2,1)S(1)} %convert_bitcast_fusion), kind=kOutput, calls=%fused_computation.84 | convolution fusion | flops 1613103104 | bytes 7733248 | tf_op jit(solution)/shard_map/mch,mth->ct/dot_general | solution.py:215
  217.8 47.7 %all-gather.14.cloned.1.call-done = bf16[512,4096]{1,0:T(8,128)(2,1)} async-done(((bf16[512,256]{1,0:T(8,128)(2,1)}), bf16[512,4096]{1,0:T(8,128)(2,1)}) %all-gather.14.cloned.1.call-update) | async-done | bytes 4194320 | tf_op jit(solution)/shard_map/all_gather | solution.py:200
  265.4 5.7 %fusion.53 = bf16[3,4096,128]{1,2,0:T(8,128)(2,1)} fusion(bf16[512,4096]{1,0:T(8,128)(2,1)} %all-gather.14.cloned.1.call-done, bf16[1,512,128]{2,1,0:T(8,128)(2,1)S(1)} %get-tuple-element.678, bf16[1,512,128]{2,1,0:T(8,128)(2,1)S(1)} %get-tuple-element.677, bf16[1,512,128]{2,1,0:T(8,128)(2,1)S(1)} %convert_bitcast_fusion), kind=kOutput, calls=%fused_computation.85 | convolution fusion | flops 1612578816 | bytes 7733248 | tf_op jit(solution)/shard_map/tc,mth->mch/dot_general | solution.py:198
  272.9 41.3 %all_to_all.16 = bf16[128,16,256]{2,0,1:T(8,128)(2,1)S(1)} all-to-all(bf16[128,16,256]{2,0,1:T(8,128)(2,1)S(1)} %copy.51), channel_id=1, replica_groups=mesh['gx'=4,'gy'=4,'gz'=2] {'gx','gy'}, dimensions={1} | all-to-all | bytes 2097152 | tf_op jit(solution)/shard_map/all_to_all | solution.py:139
  314.2 4.9 %convolution_convert_fusion.2 = bf16[16,512,256]{2,1,0:T(8,128)(2,1)} fusion(bf16[512,16,128]{0,2,1:T(8,128)(2,1)} %bitcast.189, bf16[128,16,256]{2,0,1:T(8,128)(2,1)S(1)} %all_to_all.16), kind=kOutput, calls=%fused_computation.88 | convolution fusion | flops 538968064 | bytes 7340032 | tf_op jit(solution)/shard_map/thd,hdc->htc/dot_general | solution.py:141
  322.8 12.9 %reduce-scatter.11.cloned.1.call-done = bf16[128,2048]{1,0:T(8,128)(2,1)} async-done(((bf16[128,4096]{1,0:T(8,128)(2,1)}), bf16[128,2048]{1,0:T(8,128)(2,1)}) %reduce-scatter.11.cloned.1.call-update) | async-done | bytes 524304 | tf_op jit(solution)/shard_map/reduce_scatter | solution.py:208
  337.7 74.6 %reduce-scatter.7.cloned.1.call-done = bf16[256,512]{0,1:T(8,128)(2,1)} async-done(((bf16[4096,512]{0,1:T(8,128)(2,1)}), bf16[256,512]{0,1:T(8,128)(2,1)}) %reduce-scatter.7.cloned.1.call-update) | async-done | bytes 262160 | tf_op jit(solution)/shard_map/reduce_scatter | solution.py:214
  413.6 30.6 %psum.22 = f32[512]{0:T(512)S(1)} all-reduce(f32[512]{0:T(512)S(1)} %fusion.67), channel_id=1, replica_groups=mesh['gx'=4,'gy'=4,'gz'=2] {'gx','gy'}, use_global_device_ids=true, to_apply=%region_19.20 | all-reduce | flops 512 | bytes 4096 | tf_op jit(solution)/shard_map/psum | solution.py:226
  445.6 5.7 %psum.23 = f32[2,256]{1,0:T(2,128)} all-reduce(f32[2,256]{1,0:T(2,128)S(1)} %fusion.71), channel_id=1, replica_groups=mesh['gx'=4,'gy'=4,'gz'=2] {'gz'}, use_global_device_ids=true, to_apply=%region_22.23 | all-reduce | flops 512 | bytes 4096 | tf_op jit(solution)/shard_map/psum | solution.py:232
  453.2 4.4 reduce-scatter.9.cloned.1.call-done
  (204 shorter events, 94.8 us)
Async XLA Ops:
  7.2 136.9 %all-gather.6.cloned.1.call-start = ((), (), s32[]{:S(2)}) async-start(), calls=%async_computation.5 | async-start | bytes 4718592 | tf_op jit(solution)/shard_map/all_gather | solution.py:35
  10.0 172.4 %all-gather.10.cloned.1.call-start = ((), (), s32[]{:S(2)}) async-start(), calls=%async_computation.7 | async-start | bytes 1572864 | tf_op jit(solution)/shard_map/all_gather | solution.py:36
  45.6 10.9 %collective-permute-start.1 = (bf16[512,256]{1,0:T(8,128)(2,1)S(1)}, bf16[512,256]{1,0:T(8,128)(2,1)S(1)}, u32[]{:S(2)}, u32[]{:S(2)}) collective-permute-start(bf16[512,256]{1,0:T(8,128)(2,1)S(1)} %fusion.74), channel_id=1, source_target_pairs={{0,2},{2,4},{4,6},{6,8},{8,10},{10,12},{12,14},{14,16},{16,18},{18... | collective-permute-start | bytes 786440 | tf_op jit(solution)/shard_map/ppermute | solution.py:60
  46.7 135.7 %all-gather.12.cloned.1.call-start = ((), (), s32[]{:S(2)}) async-start(), calls=%async_computation.8 | async-start | bytes 4456448 | tf_op jit(solution)/shard_map/all_gather | solution.py:149
  46.8 12.4 %collective-permute-start = (bf16[512,256]{1,0:T(8,128)(2,1)S(1)}, bf16[512,256]{1,0:T(8,128)(2,1)S(1)}, u32[]{:S(2)}, u32[]{:S(2)}) collective-permute-start(bf16[512,256]{1,0:T(8,128)(2,1)S(1)} %fusion.74), channel_id=1, source_target_pairs={{0,30},{2,0},{4,2},{6,4},{8,6},{10,8},{12,10},{14,12},{16,14},{18,... | collective-permute-start | bytes 786440 | tf_op jit(solution)/shard_map/ppermute | solution.py:62
  56.5 9.6 %collective-permute-start.3 = (bf16[512,256]{1,0:T(8,128)(2,1)S(1)}, bf16[512,256]{1,0:T(8,128)(2,1)S(1)}, u32[]{:S(2)}, u32[]{:S(2)}) collective-permute-start(bf16[512,256]{1,0:T(8,128)(2,1)S(1)} %collective-permute-done.1), channel_id=1, source_target_pairs={{0,2},{2,4},{4,6},{6,8},{8,10},{10,12},{12,14},{14,16},{16,18},{18... | collective-permute-start | bytes 786440 | tf_op jit(solution)/shard_map/ppermute | solution.py:60
  59.2 10.7 %collective-permute-start.2 = (bf16[512,256]{1,0:T(8,128)(2,1)S(1)}, bf16[512,256]{1,0:T(8,128)(2,1)S(1)}, u32[]{:S(2)}, u32[]{:S(2)}) collective-permute-start(bf16[512,256]{1,0:T(8,128)(2,1)S(1)} %collective-permute-done), channel_id=1, source_target_pairs={{0,30},{2,0},{4,2},{6,4},{8,6},{10,8},{12,10},{14,12},{16,14},{18,... | collective-permute-start | bytes 786440 | tf_op jit(solution)/shard_map/ppermute | solution.py:62
  66.1 11.3 %collective-permute-start.5 = (bf16[512,256]{1,0:T(8,128)(2,1)S(1)}, bf16[512,256]{1,0:T(8,128)(2,1)S(1)}, u32[]{:S(2)}, u32[]{:S(2)}) collective-permute-start(bf16[512,256]{1,0:T(8,128)(2,1)S(1)} %collective-permute-done.3), channel_id=1, source_target_pairs={{0,2},{2,4},{4,6},{6,8},{8,10},{10,12},{12,14},{14,16},{16,18},{18... | collective-permute-start | bytes 786440 | tf_op jit(solution)/shard_map/ppermute | solution.py:60
  69.9 13.3 %collective-permute-start.4 = (bf16[512,256]{1,0:T(8,128)(2,1)S(1)}, bf16[512,256]{1,0:T(8,128)(2,1)S(1)}, u32[]{:S(2)}, u32[]{:S(2)}) collective-permute-start(bf16[512,256]{1,0:T(8,128)(2,1)S(1)} %collective-permute-done.2), channel_id=1, source_target_pairs={{0,30},{2,0},{4,2},{6,4},{8,6},{10,8},{12,10},{14,12},{16,14},{18,... | collective-permute-start | bytes 786440 | tf_op jit(solution)/shard_map/ppermute | solution.py:62
  77.5 11.5 %collective-permute-start.7 = (bf16[512,256]{1,0:T(8,128)(2,1)S(1)}, bf16[512,256]{1,0:T(8,128)(2,1)S(1)}, u32[]{:S(2)}, u32[]{:S(2)}) collective-permute-start(bf16[512,256]{1,0:T(8,128)(2,1)S(1)} %collective-permute-done.5), channel_id=1, source_target_pairs={{0,2},{2,4},{4,6},{6,8},{8,10},{10,12},{12,14},{14,16},{16,18},{18... | collective-permute-start | bytes 786440 | tf_op jit(solution)/shard_map/ppermute | solution.py:60
  83.2 12.6 %collective-permute-start.6 = (bf16[512,256]{1,0:T(8,128)(2,1)S(1)}, bf16[512,256]{1,0:T(8,128)(2,1)S(1)}, u32[]{:S(2)}, u32[]{:S(2)}) collective-permute-start(bf16[512,256]{1,0:T(8,128)(2,1)S(1)} %collective-permute-done.4), channel_id=1, source_target_pairs={{0,30},{2,0},{4,2},{6,4},{8,6},{10,8},{12,10},{14,12},{16,14},{18,... | collective-permute-start | bytes 786440 | tf_op jit(solution)/shard_map/ppermute | solution.py:62
  89.0 9.6 %collective-permute-start.9 = (bf16[512,256]{1,0:T(8,128)(2,1)S(1)}, bf16[512,256]{1,0:T(8,128)(2,1)S(1)}, u32[]{:S(2)}, u32[]{:S(2)}) collective-permute-start(bf16[512,256]{1,0:T(8,128)(2,1)S(1)} %collective-permute-done.7), channel_id=1, source_target_pairs={{0,2},{2,4},{4,6},{6,8},{8,10},{10,12},{12,14},{14,16},{16,18},{18... | collective-permute-start | bytes 786440 | tf_op jit(solution)/shard_map/ppermute | solution.py:60
  94.2 116.7 %reduce-scatter.5.cloned.1.call-start = ((), (), s32[]{:S(2)}) async-start(), calls=%async_computation.9 | async-start | bytes 786432 | tf_op jit(solution)/shard_map/reduce_scatter | solution.py:185
  95.7 18.1 %collective-permute-start.8 = (bf16[512,256]{1,0:T(8,128)(2,1)S(1)}, bf16[512,256]{1,0:T(8,128)(2,1)S(1)}, u32[]{:S(2)}, u32[]{:S(2)}) collective-permute-start(bf16[512,256]{1,0:T(8,128)(2,1)S(1)} %collective-permute-done.6), channel_id=1, source_target_pairs={{0,30},{2,0},{4,2},{6,4},{8,6},{10,8},{12,10},{14,12},{16,14},{18,... | collective-permute-start | bytes 786440 | tf_op jit(solution)/shard_map/ppermute | solution.py:62
  98.6 19.9 %collective-permute-start.11 = (bf16[512,256]{1,0:T(8,128)(2,1)S(1)}, bf16[512,256]{1,0:T(8,128)(2,1)}, u32[]{:S(2)}, u32[]{:S(2)}) collective-permute-start(bf16[512,256]{1,0:T(8,128)(2,1)S(1)} %collective-permute-done.9), channel_id=1, source_target_pairs={{0,2},{2,4},{4,6},{6,8},{8,10},{10,12},{12,14},{14,16},{16,18},{18... | collective-permute-start | bytes 786440 | tf_op jit(solution)/shard_map/ppermute | solution.py:60
  113.8 15.2 %collective-permute-start.10 = (bf16[512,256]{1,0:T(8,128)(2,1)S(1)}, bf16[512,256]{1,0:T(8,128)(2,1)S(1)}, u32[]{:S(2)}, u32[]{:S(2)}) collective-permute-start(bf16[512,256]{1,0:T(8,128)(2,1)S(1)} %collective-permute-done.8), channel_id=1, source_target_pairs={{0,30},{2,0},{4,2},{6,4},{8,6},{10,8},{12,10},{14,12},{16,14},{18,... | collective-permute-start | bytes 786440 | tf_op jit(solution)/shard_map/ppermute | solution.py:62
  118.5 13.7 %collective-permute-start.13 = (bf16[512,256]{1,0:T(8,128)(2,1)}, bf16[512,256]{1,0:T(8,128)(2,1)}, u32[]{:S(2)}, u32[]{:S(2)}) collective-permute-start(bf16[512,256]{1,0:T(8,128)(2,1)} %collective-permute-done.11), channel_id=1, source_target_pairs={{0,2},{2,4},{4,6},{6,8},{8,10},{10,12},{12,14},{14,16},{16,18},{18... | collective-permute-start | bytes 786440 | tf_op jit(solution)/shard_map/ppermute | solution.py:60
  129.0 23.7 %collective-permute-start.12 = (bf16[512,256]{1,0:T(8,128)(2,1)S(1)}, bf16[512,256]{1,0:T(8,128)(2,1)S(1)}, u32[]{:S(2)}, u32[]{:S(2)}) collective-permute-start(bf16[512,256]{1,0:T(8,128)(2,1)S(1)} %collective-permute-done.10), channel_id=1, source_target_pairs={{0,30},{2,0},{4,2},{6,4},{8,6},{10,8},{12,10},{14,12},{16,14},{18,... | collective-permute-start | bytes 786440 | tf_op jit(solution)/shard_map/ppermute | solution.py:62
  132.2 20.8 %collective-permute-start.14 = (bf16[512,256]{1,0:T(8,128)(2,1)}, bf16[512,256]{1,0:T(8,128)(2,1)}, u32[]{:S(2)}, u32[]{:S(2)}) collective-permute-start(bf16[512,256]{1,0:T(8,128)(2,1)} %collective-permute-done.13), channel_id=1, source_target_pairs={{0,2},{2,4},{4,6},{6,8},{8,10},{10,12},{12,14},{14,16},{16,18},{18... | collective-permute-start | bytes 786440 | tf_op jit(solution)/shard_map/ppermute | solution.py:60
  196.6 68.8 %all-gather.14.cloned.1.call-start = ((), (), s32[]{:S(2)}) async-start(), calls=%async_computation.11 | async-start | bytes 4456448 | tf_op jit(solution)/shard_map/all_gather | solution.py:200
  197.2 117.0 %all-gather.8.cloned.1.call-start = ((), (), s32[]{:S(2)}) async-start(), calls=%async_computation.6 | async-start | bytes 2228224 | tf_op jit(solution)/shard_map/all_gather | solution.py:138
  197.8 137.8 %reduce-scatter.11.cloned.1.call-start = ((), (), s32[]{:S(2)}) async-start(), calls=%async_computation.13 | async-start | bytes 1572864 | tf_op jit(solution)/shard_map/reduce_scatter | solution.py:208
  201.8 210.5 %reduce-scatter.7.cloned.1.call-start = ((), (), s32[]{:S(2)}) async-start(), calls=%async_computation.10 | async-start | bytes 4456448 | tf_op jit(solution)/shard_map/reduce_scatter | solution.py:214
  217.7 239.9 %reduce-scatter.9.cloned.1.call-start = ((), (), s32[]{:S(2)}) async-start(), calls=%async_computation.12 | async-start | bytes 4718592 | tf_op jit(solution)/shard_map/reduce_scatter | solution.py:205
  (19 other events, 832.4 us)
Sparse Core Ops, SparseCore 0:
  10.1 47.6 all-gather.5
  59.9 21.2 all-gather.9
  94.4 75.1 all-gather.11
  196.8 14.1 reduce-scatter.4
  212.9 52.4 all-gather.13
  268.1 45.3 all-gather.7
  316.3 19.3 reduce-scatter.10
  339.5 72.7 reduce-scatter.6
  415.1 42.4 reduce-scatter.8
